TPU v7x, 32 devices: a whole 2x2x4 slice. The times are simulated.
32 devices in a mesh: dp: 8 (over y, x, core), mp: 4 (over z).
Axes of the slice: x: 2, y: 2, z: 4, core: 2. Of those that a mesh axis runs over, the one named last changes fastest.
Arguments:
- feature_ids: int32 [8, 2048, 8], P('dp'), may hold values from 0 to 4095
- tables: bfloat16 [8, 4096, 128], P('dp'), may hold values from -5 to 5
- table_of_feature: int32 [8], replicated, may hold values from 0 to 7, each once
- cross_down: bfloat16 [2, 1024, 512], P(None, 'mp'), may hold values from -0.1875 to 0.1875
- cross_up: bfloat16 [2, 1024, 512], P(None, 'mp'), may hold values from -0.125 to 0.125
- cross_bias: float32 [2, 1024], P(None, 'mp'), may hold values from -3 to 3
- tower_weight: bfloat16 [1024, 2048], P('dp', 'mp'), may hold values from -0.1875 to 0.1875
- tower_bias: float32 [2048], P('mp'), may hold values from -3 to 3
Outputs:
- hidden: bfloat16 [2048, 2048], P('dp', 'mp')
Inputs may be any that keep to these rules, and one draw needn't show every extreme that they name: `feature_ids`: each id indexes a row of its own table. `table_of_feature`: each table serves exactly one feature.
All inputs are finite; a program needn't handle non-finite values.
Results may differ from a plain program's by a relative error of at most 0.015.
Values may be sent and summed in bfloat16 or wider, within the bound.
A program may use at most 64 MiB of HBM per device.

v0:
```python
import jax
import jax.numpy as jnp
from jax import lax
from jax.sharding import PartitionSpec as P


def body(
    feature_ids,
    tables,
    table_of_feature,
    cross_down,
    cross_up,
    cross_bias,
    tower_weight,
    tower_bias,
):
    groups = lax.axis_size("dp")
    members = lax.axis_size("mp")
    member = lax.axis_index("mp")
    table_count, batch_size, hot_count = feature_ids.shape
    row_count = batch_size // (groups * members)
    shaped = feature_ids[0].reshape(groups, members, row_count, hot_count)
    own_ids = lax.dynamic_index_in_dim(shaped, member, 1, keepdims=False).reshape(
        groups * row_count, hot_count
    )
    summed = jnp.zeros((groups * row_count, tables.shape[2]), jnp.float32)
    for hot_index in range(hot_count):
        summed = summed + jnp.take(tables[0], own_ids[:, hot_index], axis=0).astype(jnp.float32)
    columns = [summed.astype(jnp.bfloat16)]
    pooled = jnp.stack(columns, axis=1)
    regrouped = lax.all_to_all(pooled, "dp", split_axis=0, concat_axis=1, tiled=True)
    ordered = jnp.take(regrouped, table_of_feature, axis=1)
    by_width = lax.all_to_all(ordered, "mp", split_axis=1, concat_axis=0, tiled=True)
    group_rows = by_width.shape[0]
    embedded = by_width.reshape(group_rows, -1)
    embedded_wide = embedded.astype(jnp.float32)
    crossed = embedded
    layer_total = cross_down.shape[0]
    for layer_index in range(layer_total):
        partial_value = jnp.dot(
            crossed, cross_down[layer_index], preferred_element_type=jnp.float32
        )
        projected = lax.psum(partial_value.astype(jnp.bfloat16), "mp")
        lifted = lax.dot_general(
            projected,
            cross_up[layer_index],
            (((1,), (1,)), ((), ())),
            preferred_element_type=jnp.float32,
        )
        crossed = (
            embedded_wide * (lifted + cross_bias[layer_index]) + crossed.astype(jnp.float32)
        ).astype(jnp.bfloat16)
    full_rows = lax.all_gather(crossed, "mp", axis=1, tiled=True)
    pre_act = jnp.dot(
        full_rows,
        lax.all_gather(tower_weight, "dp", axis=0, tiled=True),
        preferred_element_type=jnp.float32,
    )
    return jax.nn.relu(pre_act + tower_bias).astype(jnp.bfloat16)


def solution(mesh):
    return jax.shard_map(
        body,
        mesh=mesh,
        in_specs=(
            P("dp", None, None),
            P("dp", None, None),
            P(),
            P(None, "mp", None),
            P(None, "mp", None),
            P(None, "mp"),
            P("dp", "mp"),
            P("mp"),
        ),
        out_specs=P("dp", "mp"),
        check_vma=False,
    )
```

profile of v0, /device:TPU:0, one launch (start us, length us, event | category | flops | bytes accessed | tf_op | source)
XLA Modules:
  0.0 143.6 jit_solution(9518459660529289800)
XLA Ops:
  7.4 0.0 copy-start
  7.4 1.0 reshape_squeeze.3
  8.4 0.1 dynamic-slice_reduce_fusion
  8.5 0.1 reshape.19
  8.8 0.0 copy-done
  8.8 1.3 gather_fusion.2
  10.2 1.3 gather_fusion.3
  11.5 1.3 gather_fusion.4
  12.9 1.3 gather_fusion.5
  14.2 1.3 gather_fusion.6
  15.6 1.3 gather_fusion.7
  17.0 1.3 gather_fusion.8
  18.3 1.3 gather_fusion.1
  19.7 0.8 fusion.16
  20.5 0.5 broadcast.59
  21.0 0.7 reduce.4
  21.7 0.7 reshape.125
  22.3 0.0 copy-start.5
  22.3 5.3 %all-to-all-start = ((bf16[8,2,4096]{2,1,0:T(2,128)(2,1)}), bf16[8,2,4096]{2,1,0:T(2,128)(2,1)S(1)}, u32[]{:S(2)}, u32[]{:S(2)}) async-start(bf16[8,2,4096]{2,1,0:T(2,128)(2,1)} %reshape.125), calls=%async_computation | async-start | bytes 262144 | tf_op jit(solution)/shard_map/all_to_all | solution.py:31
  27.7 0.0 all-reduce.3.cloned.1.call-start
  27.7 0.0 copy-done.5
  27.8 5.4 %all-to-all-done = bf16[8,2,4096]{2,1,0:T(2,128)(2,1)S(1)} async-done(((bf16[8,2,4096]{2,1,0:T(2,128)(2,1)}), bf16[8,2,4096]{2,1,0:T(2,128)(2,1)S(1)}, u32[]{:S(2)}, u32[]{:S(2)}) %all-to-all-start) | async-done | bytes 131104 | tf_op jit(solution)/shard_map/all_to_all | solution.py:31
  33.2 0.1 reshape.126
  33.3 0.0 copy-start.1
  33.3 0.6 gather_fusion
  33.9 0.1 select_bitcast_fusion
  34.0 10.6 %all_to_all.33 = bf16[64,8,128]{2,0,1:T(8,128)(2,1)S(1)} all-to-all(bf16[64,8,128]{2,0,1:T(8,128)(2,1)S(1)} %select_bitcast_fusion), channel_id=1, replica_groups=mesh['dp'=8,'mp'=4] {'mp'}, dimensions={1} | all-to-all | bytes 262144 | tf_op jit(solution)/shard_map/all_to_all | solution.py:33
  44.6 0.1 copy.13
  44.8 0.0 copy-start.3
  44.8 0.0 copy-done.1
  44.8 0.9 convolution_convert_fusion.1
  45.7 0.0 copy-start.2
  45.7 0.0 all-reduce.3.cloned.1.call-update
  45.8 0.0 all-reduce.5.cloned.1.call-start
  45.8 0.6 copy-done.2
  46.4 32.4 %all-reduce.3.cloned.1.call-done = bf16[256,512]{1,0:T(8,128)(2,1)} async-done(((bf16[256,512]{1,0:T(8,128)(2,1)}), bf16[256,512]{1,0:T(8,128)(2,1)}) %all-reduce.3.cloned.1.call-update) | async-done | bytes 262160 | tf_op jit(solution)/shard_map/psum | solution.py:43
  78.8 0.0 copy-done.3
  78.8 1.2 fusion.6
  80.0 0.9 convolution_convert_fusion
  80.9 0.0 all-reduce.5.cloned.1.call-update
  81.0 0.0 all-gather.2.cloned.1.call-start
  81.0 0.5 all-gather.2.cloned.1.call-update
  81.5 35.1 %all-reduce.5.cloned.1.call-done = bf16[256,512]{1,0:T(8,128)(2,1)} async-done(((bf16[256,512]{1,0:T(8,128)(2,1)}), bf16[256,512]{1,0:T(8,128)(2,1)}) %all-reduce.5.cloned.1.call-update) | async-done | bytes 262160 | tf_op jit(solution)/shard_map/psum | solution.py:43
  116.6 1.2 fusion.7
  117.8 0.0 copy-start.4
  117.8 16.0 %all_gather.6 = bf16[256,1024]{1,0:T(8,128)(2,1)S(1)} all-gather(bf16[256,256]{1,0:T(8,128)(2,1)S(1)} %fusion.7), channel_id=1, replica_groups=mesh['dp'=8,'mp'=4] {'mp'}, dimensions={1}, use_global_device_ids=true | all-gather | bytes 655360 | tf_op jit(solution)/shard_map/all_gather | solution.py:53
  133.8 0.0 copy-done.4
  133.8 2.4 %fusion.1 = bf16[256,512]{1,0:T(8,128)(2,1)} fusion(bf16[256,1024]{1,0:T(8,128)(2,1)S(1)} %all_gather.6, bf16[1024,512]{1,0:T(8,128)(2,1)} %all-gather.2.cloned.1.call-done, f32[512]{0:T(512)S(1)} %copy-done.4), kind=kOutput, calls=%fused_computation.11 | convolution fusion | flops 268828672 | bytes 1837056 | tf_op jit(solution)/shard_map/dot_general | solution.py:54
  (27 shorter events, 0.2 us)
Async XLA Ops:
  7.4 1.4 %copy-start = (bf16[1,4096,128]{2,1,0:T(8,128)(2,1)S(1)}, bf16[1,4096,128]{2,1,0:T(8,128)(2,1)}, u32[]{:S(2)}) copy-start(bf16[1,4096,128]{2,1,0:T(8,128)(2,1)} %param.11) | copy-start | bytes 3145732
  22.3 5.4 %copy-start.5 = (s32[8]{0:T(128)S(1)}, s32[8]{0:T(128)}, u32[]{:S(2)}) copy-start(s32[8]{0:T(128)} %param.12) | copy-start | bytes 100
  22.3 10.8 %all-to-all-start = ((bf16[8,2,4096]{2,1,0:T(2,128)(2,1)}), bf16[8,2,4096]{2,1,0:T(2,128)(2,1)S(1)}, u32[]{:S(2)}, u32[]{:S(2)}) async-start(bf16[8,2,4096]{2,1,0:T(2,128)(2,1)} %reshape.125), calls=%async_computation | async-start | bytes 262144 | tf_op jit(solution)/shard_map/all_to_all | solution.py:31
  27.7 51.1 %all-reduce.3.cloned.1.call-start = ((), (), s32[]{:S(2)}) async-start(), calls=%async_computation.2 | async-start | bytes 524288 | tf_op jit(solution)/shard_map/psum | solution.py:43
  33.3 11.5 %copy-start.1 = (bf16[2,256,512]{2,1,0:T(8,128)(2,1)S(1)}, bf16[2,256,512]{2,1,0:T(8,128)(2,1)}, u32[]{:S(2)}) copy-start(bf16[2,256,512]{2,1,0:T(8,128)(2,1)} %param.13) | copy-start | bytes 1572868
  44.8 34.0 %copy-start.3 = (bf16[2,256,512]{2,1,0:T(8,128)(2,1)S(1)}, bf16[2,256,512]{2,1,0:T(8,128)(2,1)}, u32[]{:S(2)}) copy-start(bf16[2,256,512]{2,1,0:T(8,128)(2,1)} %param.14) | copy-start | bytes 1572868
  45.7 0.7 copy-start.2
  45.8 70.8 %all-reduce.5.cloned.1.call-start = ((), (), s32[]{:S(2)}) async-start(), calls=%async_computation.3 | async-start | bytes 524288 | tf_op jit(solution)/shard_map/psum | solution.py:43
  81.0 52.8 %all-gather.2.cloned.1.call-start = ((), (), s32[]{:S(2)}) async-start(), calls=%async_computation.4 | async-start | bytes 1179648 | tf_op jit(solution)/shard_map/all_gather | solution.py:56
  117.8 16.0 %copy-start.4 = (f32[512]{0:T(512)S(1)}, f32[512]{0:T(512)}, u32[]{:S(2)}) copy-start(f32[512]{0:T(512)} %param.17) | copy-start | bytes 6148
Sparse Core Ops, SparseCore 0:
  45.9 32.8 all-reduce.2
  81.1 35.4 all-reduce.4
Sparse Core Ops, SparseCore 1:
  83.3 23.1 all-gather.1
where the time goes:
time: 144 us
  waiting for transfers between devices  73.4 us (51%)
  blocking collectives  26.6 us (18%)
  between operations  15.2 us (11%)
  local copies, waits for them, and re-layouts  14.7 us (10%)
  matrix products  6.65 us (5%)
  starting transfers between devices  5.45 us (4%)
  other arithmetic  1.66 us (1%)
    psum x2, waiting for transfers between devices, body(): projected = lax.psum(partial_value.astype(jnp.bfloat16), 'mp')  67.4 us
    all_gather x1, blocking collectives, body(): full_rows = lax.all_gather(crossed, 'mp', axis=1, tiled=True)  16 us
    gather x8, local copies, waits for them, and re-layouts, body(): jnp.take(tables[0], own_ids[:, hot_index], axis=0).astype(jnp.float32)  10.7 us
    all_to_all x1, blocking collectives, body(): lax.all_to_all(ordered, 'mp', split_axis=1, concat_axis=0, tiled=True)  10.6 us
    all_to_all x1, waiting for transfers between devices, body(): lax.all_to_all(pooled, 'dp', split_axis=0, concat_axis=1, tiled=True)  5.4 us
    all_to_all x1, starting transfers between devices, body(): lax.all_to_all(pooled, 'dp', split_axis=0, concat_axis=1, tiled=True)  5.33 us
  transfers between devices with their start and end apart: 4, of which 3 were waited for; matrix products, arithmetic and copies ran while one was open for 1% of the time, Pallas kernels for 0%

commit v1 on v0

--- a/solution.py
+++ b/solution.py
@@ -2,6 +2,11 @@
 import jax.numpy as jnp
 from jax import lax
 from jax.sharding import PartitionSpec as P
+
+
+def run_figure_now(u_in, a_name):
+    n_now = jnp.sum(lax.all_gather(u_in, a_name), axis=0)
+    return n_now
 
 
 def body(
@@ -40,7 +45,7 @@
         partial_value = jnp.dot(
             crossed, cross_down[layer_index], preferred_element_type=jnp.float32
         )
-        projected = lax.psum(partial_value.astype(jnp.bfloat16), "mp")
+        projected = run_figure_now(partial_value.astype(jnp.bfloat16), "mp")
         lifted = lax.dot_general(
             projected,
             cross_up[layer_index],

time: 144 us -> 135 us (0.938)
  waiting for transfers between devices: 73.4 us -> 65.3 us
  other arithmetic: 1.66 us -> 4.62 us
  matrix products: 6.65 us -> 4.76 us
  between operations: 15.2 us -> 13.5 us
    psum x2 -> x0, waiting for transfers between devices: 67.4 us -> none  [body(): projected = lax.psum(partial_value.astype(jnp.bfloat16), 'mp')]
    all_gather x0 -> x2, waiting for transfers between devices: none -> 51.5 us  [run_figure_now(): n_now = jnp.sum(lax.all_gather(u_in, a_name), axis=0)]
    all_gather x1, waiting for transfers between devices: 0.01 us -> 7.64 us  [body(): lax.all_gather(tower_weight, 'dp', axis=0, tiled=True)]
    reduce_sum x0 -> x2, other arithmetic: none -> 2.96 us  [run_figure_now(): n_now = jnp.sum(lax.all_gather(u_in, a_name), axis=0)]
    dot_general x2, matrix products: 2.42 us -> 0.52 us  [body(): lax.dot_general(projected, cross_up[layer_index], (((1,), (1,)), ((), ())...]
  transfers between devices with their start and end apart: 4 -> 4, of which waited for: 3 -> 4; matrix products, arithmetic and copies ran while one was open for 1% -> 1% of each run, Pallas kernels for 0% -> 0%
where the time goes in v1:
time: 135 us; the launch traced here: 134 us
  waiting for transfers between devices  65.3 us (48%)
  blocking collectives  25.9 us (19%)
  local copies, waits for them, and re-layouts  14.6 us (11%)
  between operations  13.5 us (10%)
  starting transfers between devices  5.45 us (4%)
  matrix products  4.76 us (4%)
  other arithmetic  4.62 us (3%)
    all_gather x2, waiting for transfers between devices, run_figure_now(): n_now = jnp.sum(lax.all_gather(u_in, a_name), axis=0)  51.5 us
    all_gather x1, blocking collectives, body(): full_rows = lax.all_gather(crossed, 'mp', axis=1, tiled=True)  15.3 us
    gather x8, local copies, waits for them, and re-layouts, body(): jnp.take(tables[0], own_ids[:, hot_index], axis=0).astype(jnp.float32)  10.7 us
    all_to_all x1, blocking collectives, body(): lax.all_to_all(ordered, 'mp', split_axis=1, concat_axis=0, tiled=True)  10.6 us
    all_gather x1, waiting for transfers between devices, body(): lax.all_gather(tower_weight, 'dp', axis=0, tiled=True)  7.64 us
    all_to_all x1, waiting for transfers between devices, body(): lax.all_to_all(pooled, 'dp', split_axis=0, concat_axis=1, tiled=True)  5.4 us
    all_to_all x1, starting transfers between devices, body(): lax.all_to_all(pooled, 'dp', split_axis=0, concat_axis=1, tiled=True)  5.33 us
    reduce_sum x2, other arithmetic, run_figure_now(): n_now = jnp.sum(lax.all_gather(u_in, a_name), axis=0)  2.96 us
  transfers between devices with their start and end apart: 4, of which 4 were waited for; matrix products, arithmetic and copies ran while one was open for 1% of the time, Pallas kernels for 0%

profile of v1, /device:TPU:0, one launch (start us, length us, event | category | flops | bytes accessed | tf_op | source)
XLA Modules:
  0.0 134.2 jit_solution(10612441284163100651)
XLA Ops:
  6.5 0.0 copy-start
  6.5 1.0 reshape_squeeze.3
  7.6 0.1 dynamic-slice_reduce_fusion
  7.7 0.1 reshape.19
  8.0 0.0 copy-done
  8.0 1.3 gather_fusion.2
  9.3 1.3 gather_fusion.3
  10.7 1.3 gather_fusion.4
  12.1 1.3 gather_fusion.5
  13.4 1.3 gather_fusion.6
  14.8 1.3 gather_fusion.7
  16.1 1.3 gather_fusion.8
  17.5 1.3 gather_fusion.1
  18.9 0.8 fusion.16
  19.6 0.5 broadcast.59
  20.1 0.7 reduce.6
  20.8 0.7 reshape.127
  21.5 5.3 %all-to-all-start = ((bf16[8,2,4096]{2,1,0:T(2,128)(2,1)}), bf16[8,2,4096]{2,1,0:T(2,128)(2,1)S(1)}, u32[]{:S(2)}, u32[]{:S(2)}) async-start(bf16[8,2,4096]{2,1,0:T(2,128)(2,1)} %reshape.127), calls=%async_computation | async-start | bytes 262144 | tf_op jit(solution)/shard_map/all_to_all | solution.py:36
  26.8 0.0 all-gather.8.cloned.1.call-start
  26.9 0.0 copy-done.5
  26.9 5.4 %all-to-all-done = bf16[8,2,4096]{2,1,0:T(2,128)(2,1)S(1)} async-done(((bf16[8,2,4096]{2,1,0:T(2,128)(2,1)}), bf16[8,2,4096]{2,1,0:T(2,128)(2,1)S(1)}, u32[]{:S(2)}, u32[]{:S(2)}) %all-to-all-start) | async-done | bytes 131104 | tf_op jit(solution)/shard_map/all_to_all | solution.py:36
  32.3 0.1 reshape.128
  32.5 0.0 copy-start.1
  32.5 0.6 gather_fusion
  33.1 0.1 select_bitcast_fusion
  33.2 10.6 %all_to_all.33 = bf16[64,8,128]{2,0,1:T(8,128)(2,1)S(1)} all-to-all(bf16[64,8,128]{2,0,1:T(8,128)(2,1)S(1)} %select_bitcast_fusion), channel_id=1, replica_groups=mesh['dp'=8,'mp'=4] {'mp'}, dimensions={1} | all-to-all | bytes 262144 | tf_op jit(solution)/shard_map/all_to_all | solution.py:38
  43.8 0.1 copy.13
  44.0 0.0 copy-done.1
  44.0 0.9 convolution_convert_fusion.1
  44.9 0.0 all-gather.8.cloned.1.call-update
  44.9 0.0 all-gather.10.cloned.1.call-start
  45.0 0.6 copy-done.2
  45.6 24.7 %all-gather.8.cloned.1.call-done = bf16[1024,512]{1,0:T(8,128)(2,1)} async-done(((bf16[256,512]{1,0:T(8,128)(2,1)}), bf16[1024,512]{1,0:T(8,128)(2,1)}) %all-gather.8.cloned.1.call-update) | async-done | bytes 1048592 | tf_op jit(solution)/shard_map/all_gather | solution.py:8
  70.3 1.5 %reduce_sum.24 = bf16[256,512]{1,0:T(8,128)(2,1)S(1)} reduce(bf16[4,256,512]{2,1,0:T(8,128)(2,1)} %bitcast.62, bf16[]{:T(256)} %constant.40.clone.1), dimensions={0}, to_apply=%region_0.2 | reduce | flops 393216 | bytes 1310722 | tf_op jit(solution)/shard_map/reduce_sum | solution.py:8
  71.8 0.0 copy-done.3
  71.8 0.3 fusion.6
  72.1 0.9 convolution_convert_fusion
  73.0 0.0 all-gather.10.cloned.1.call-update
  73.1 0.0 all-gather.6.cloned.1.call-start
  73.1 0.7 all-gather.6.cloned.1.call-update
  73.8 26.8 %all-gather.10.cloned.1.call-done = bf16[1024,512]{1,0:T(8,128)(2,1)} async-done(((bf16[256,512]{1,0:T(8,128)(2,1)}), bf16[1024,512]{1,0:T(8,128)(2,1)}) %all-gather.10.cloned.1.call-update) | async-done | bytes 1048592 | tf_op jit(solution)/shard_map/all_gather | solution.py:8
  100.6 1.5 %reduce_sum.25 = bf16[256,512]{1,0:T(8,128)(2,1)S(1)} reduce(bf16[4,256,512]{2,1,0:T(8,128)(2,1)} %bitcast.61, bf16[]{:T(256)} %constant.40.clone.1), dimensions={0}, to_apply=%region_1.3 | reduce | flops 393216 | bytes 1310722 | tf_op jit(solution)/shard_map/reduce_sum | solution.py:8
  102.0 0.3 fusion.7
  102.3 0.0 copy-start.4
  102.3 15.3 %all_gather.22 = bf16[256,1024]{1,0:T(8,128)(2,1)S(1)} all-gather(bf16[256,256]{1,0:T(8,128)(2,1)S(1)} %fusion.7), channel_id=1, replica_groups=mesh['dp'=8,'mp'=4] {'mp'}, dimensions={1}, use_global_device_ids=true | all-gather | bytes 655360 | tf_op jit(solution)/shard_map/all_gather | solution.py:58
  117.6 7.6 %all-gather.6.cloned.1.call-done = bf16[1024,512]{1,0:T(8,128)(2,1)} async-done(((bf16[128,512]{1,0:T(8,128)(2,1)}), bf16[1024,512]{1,0:T(8,128)(2,1)}) %all-gather.6.cloned.1.call-update) | async-done | bytes 1048592 | tf_op jit(solution)/shard_map/all_gather | solution.py:61
  125.3 0.0 copy-done.4
  125.3 2.4 %fusion.1 = bf16[256,512]{1,0:T(8,128)(2,1)} fusion(bf16[256,1024]{1,0:T(8,128)(2,1)S(1)} %all_gather.22, bf16[1024,512]{1,0:T(8,128)(2,1)} %all-gather.6.cloned.1.call-done, f32[512]{0:T(512)S(1)} %copy-done.4), kind=kOutput, calls=%fused_computation.11 | convolution fusion | flops 268828672 | bytes 1837056 | tf_op jit(solution)/shard_map/dot_general | solution.py:59
  (29 shorter events, 0.2 us)
Async XLA Ops:
  6.5 1.4 %copy-start = (bf16[1,4096,128]{2,1,0:T(8,128)(2,1)S(1)}, bf16[1,4096,128]{2,1,0:T(8,128)(2,1)}, u32[]{:S(2)}) copy-start(bf16[1,4096,128]{2,1,0:T(8,128)(2,1)} %param.11) | copy-start | bytes 3145732
  21.5 5.4 %copy-start.5 = (s32[8]{0:T(128)S(1)}, s32[8]{0:T(128)}, u32[]{:S(2)}) copy-start(s32[8]{0:T(128)} %param.12) | copy-start | bytes 100
  21.5 10.8 %all-to-all-start = ((bf16[8,2,4096]{2,1,0:T(2,128)(2,1)}), bf16[8,2,4096]{2,1,0:T(2,128)(2,1)S(1)}, u32[]{:S(2)}, u32[]{:S(2)}) async-start(bf16[8,2,4096]{2,1,0:T(2,128)(2,1)} %reshape.127), calls=%async_computation | async-start | bytes 262144 | tf_op jit(solution)/shard_map/all_to_all | solution.py:36
  26.8 43.5 %all-gather.8.cloned.1.call-start = ((), (), s32[]{:S(2)}) async-start(), calls=%async_computation.3 | async-start | bytes 1310720 | tf_op jit(solution)/shard_map/all_gather | solution.py:8
  32.5 11.5 %copy-start.1 = (bf16[2,256,512]{2,1,0:T(8,128)(2,1)S(1)}, bf16[2,256,512]{2,1,0:T(8,128)(2,1)}, u32[]{:S(2)}) copy-start(bf16[2,256,512]{2,1,0:T(8,128)(2,1)} %param.13) | copy-start | bytes 1572868
  44.9 0.7 copy-start.2
  44.9 55.7 %all-gather.10.cloned.1.call-start = ((), (), s32[]{:S(2)}) async-start(), calls=%async_computation.4 | async-start | bytes 1310720 | tf_op jit(solution)/shard_map/all_gather | solution.py:8
  70.3 1.5 %copy-start.3 = (bf16[2,256,512]{2,1,0:T(8,128)(2,1)S(1)}, bf16[2,256,512]{2,1,0:T(8,128)(2,1)}, u32[]{:S(2)}) copy-start(bf16[2,256,512]{2,1,0:T(8,128)(2,1)} %param.14) | copy-start | bytes 1572868
  73.1 52.2 %all-gather.6.cloned.1.call-start = ((), (), s32[]{:S(2)}) async-start(), calls=%async_computation.2 | async-start | bytes 1179648 | tf_op jit(solution)/shard_map/all_gather | solution.py:61
  102.3 23.0 %copy-start.4 = (f32[512]{0:T(512)S(1)}, f32[512]{0:T(512)}, u32[]{:S(2)}) copy-start(f32[512]{0:T(512)} %param.17) | copy-start | bytes 6148
Sparse Core Ops, SparseCore 0:
  45.0 25.2 all-gather.7
  73.2 27.3 all-gather.9
  102.5 22.7 all-gather.5
